TPU v7x, 256 devices: a whole 4x4x8 slice. The times are simulated.
256 devices in a mesh: replica: 16 (over z_lo, y, core), model: 16 (over z_hi, x).
Axes of the slice: x: 4, y: 4, z: 8 (z_hi: 4, z_lo: 2; z = z_hi * 2 + z_lo), core: 2. Of those that a mesh axis runs over, the one named last changes fastest.
Arguments:
- partial_query: float32 [16, 2048, 2048], P('replica', None, 'model'), may hold values from -4 to 4
- partial_key: float32 [16, 2048, 2048], P('replica', None, 'model'), may hold values from -4 to 4
- partial_value: float32 [16, 2048, 2048], P('replica', None, 'model'), may hold values from -4 to 4
- partial_mixed: float32 [16, 2048, 2048], P('replica', 'model'), may hold values from -4 to 4
- partial_norm: float32 [16, 2048], P('replica'), may hold values from -8 to 8
- partial_bias: float32 [16, 2048], P('replica'), may hold values from -8 to 8
- master_query: float32 [2048, 2048], P('replica', 'model'), may hold values from -0.1875 to 0.1875
- master_key: float32 [2048, 2048], P('replica', 'model'), may hold values from -0.1875 to 0.1875
- master_value: float32 [2048, 2048], P('replica', 'model'), may hold values from -0.1875 to 0.1875
- master_mixed: float32 [2048, 2048], P('model', 'replica'), may hold values from -0.1875 to 0.1875
- master_norm: float32 [2048], P('replica'), may hold values from 0.25 to 1.75
- master_bias: float32 [2048], P('replica'), may hold values from -3 to 3
- memory_query: float32 [2048, 2048], P('replica', 'model'), may hold values from 9.765625e-05 to 0.0009765625
- memory_key: float32 [2048, 2048], P('replica', 'model'), may hold values from 9.765625e-05 to 0.0009765625
- memory_value: float32 [2048, 2048], P('replica', 'model'), may hold values from 9.765625e-05 to 0.0009765625
- memory_mixed: float32 [2048, 2048], P('model', 'replica'), may hold values from 9.765625e-05 to 0.0009765625
- memory_norm: float32 [2048], P('replica'), may hold values from 0.05 to 0.8
- memory_bias: float32 [2048], P('replica'), may hold values from 0.05 to 0.8
Outputs:
- compute_query: bfloat16 [2048, 2048], P(None, 'model')
- compute_key: bfloat16 [2048, 2048], P(None, 'model')
- compute_value: bfloat16 [2048, 2048], P(None, 'model')
- compute_mixed: bfloat16 [2048, 2048], P('model')
- compute_norm: bfloat16 [2048], replicated
- compute_bias: bfloat16 [2048], replicated
- stepped_query: float32 [2048, 2048], P('replica', 'model')
- stepped_key: float32 [2048, 2048], P('replica', 'model')
- stepped_value: float32 [2048, 2048], P('replica', 'model')
- stepped_mixed: float32 [2048, 2048], P('model', 'replica')
- stepped_norm: float32 [2048], P('replica')
- stepped_bias: float32 [2048], P('replica')
- state_new_query: float32 [2048, 2048], P('replica', 'model')
- state_new_key: float32 [2048, 2048], P('replica', 'model')
- state_new_value: float32 [2048, 2048], P('replica', 'model')
- state_new_mixed: float32 [2048, 2048], P('model', 'replica')
- state_new_norm: float32 [2048], P('replica')
- state_new_bias: float32 [2048], P('replica')
All inputs are finite; a program needn't handle non-finite values.
Results may differ from a plain program's by a relative error of at most 0.0004.
Values may be sent and summed in bfloat16 or wider, within the bound.
A program may use at most 64 MiB of HBM per device.

v0:
```python
import jax
import jax.numpy as jnp
from jax import lax
from jax.sharding import Mesh
from jax.sharding import PartitionSpec as P

REPLICA = ("replica_0", "replica_1", "replica_2")
learn_rate = 0.015
hold_rate = 0.8


def cut_along(x, dim, size):
    before, after = (x.shape[:dim], x.shape[dim + 1 :])
    return jnp.moveaxis(x.reshape(*before, size, -1, *after), dim, 0)


def sum_at_owner(x, axis, dim):
    size = lax.axis_size(axis)
    blocks = lax.all_to_all(cut_along(x, dim, size), axis, 0, 0, tiled=True)
    return jnp.sum(blocks, axis=0)


def sum_by_axis(x, axes, dim):
    far, near = axes
    own = sum_at_owner(cut_along(x, dim, lax.axis_size(far)), near, dim + 1)
    return jnp.sum(lax.all_to_all(own, far, 0, 0, tiled=True), axis=0)


def in_one_piece(arrays, axis, dim, along):
    widths = [a.shape[along] for a in arrays]
    both = jnp.concatenate(arrays, axis=along)
    out = sum_by_axis(both, axis, dim)
    return tuple(jnp.split(out, [sum(widths[:k]) for k in range(1, len(widths))], axis=along))


def copy_for_each(x, axis):
    copies = jnp.broadcast_to(x, (lax.axis_size(axis), *x.shape))
    return lax.all_to_all(copies, axis, split_axis=0, concat_axis=0, tiled=True)


def of_everyone(x, axis):
    return copy_for_each(x, axis).sum(axis=0)


def together(arrays, axis):
    ends = [0]
    for a in arrays:
        ends.append(ends[-1] + a.size)
    subtotal = of_everyone(jnp.concatenate([a.ravel() for a in arrays]), axis)
    return tuple((subtotal[b:e].reshape(a.shape) for a, b, e in zip(arrays, ends, ends[1:])))


def gather_turned(arrays, axis, dims):
    turned = [jnp.moveaxis(a, dim, 0) for a, dim in zip(arrays, dims)]
    both = jnp.concatenate([t.reshape(len(t), -1) for t in turned], axis=1)
    out, at, outs = (lax.all_gather(both, axis, axis=0, tiled=True), 0, [])
    for t, dim in zip(turned, dims):
        share = out[:, at : at + t[0].size].reshape(-1, *t.shape[1:])
        outs.append(jnp.moveaxis(share, 0, dim))
        at += t[0].size
    return tuple(outs)


def shards(
    partial_query,
    partial_key,
    partial_value,
    partial_mixed,
    partial_norm,
    partial_bias,
    master_query,
    master_key,
    master_value,
    master_mixed,
    master_norm,
    master_bias,
    memory_query,
    memory_key,
    memory_value,
    memory_mixed,
    memory_norm,
    memory_bias,
):
    mean_query, mean_key, mean_value, mean_mixed, mean_norm, mean_bias = (
        *in_one_piece(
            (partial_query[0], partial_key[0], partial_value[0]),
            (("replica_0", "replica_1"), "replica_2"),
            0,
            1,
        ),
        sum_by_axis(partial_mixed[0], (("replica_0", "replica_1"), "replica_2"), 1),
        sum_by_axis(partial_norm[0], (("replica_0", "replica_1"), "replica_2"), 0),
        sum_by_axis(partial_bias[0], (("replica_0", "replica_1"), "replica_2"), 0),
    )
    mean_rate = lax.axis_size(REPLICA) ** (-0.5)
    mean_query = mean_query * mean_rate
    mean_key = mean_key * mean_rate
    mean_value = mean_value * mean_rate
    mean_mixed = mean_mixed * mean_rate
    mean_norm = mean_norm * mean_rate
    mean_bias = mean_bias * mean_rate
    (
        own_query,
        own_key,
        own_value,
        own_mixed,
        slope_query_norm,
        slope_key_norm,
        slope_value_norm,
        slope_mixed_norm,
    ) = together(
        (
            jnp.sum(master_query * master_query, axis=1, keepdims=True),
            jnp.sum(master_key * master_key, axis=1, keepdims=True),
            jnp.sum(master_value * master_value, axis=1, keepdims=True),
            jnp.sum(master_mixed * master_mixed, axis=0, keepdims=True),
            jnp.sum(mean_query * mean_query, axis=1, keepdims=True),
            jnp.sum(mean_key * mean_key, axis=1, keepdims=True),
            jnp.sum(mean_value * mean_value, axis=1, keepdims=True),
            jnp.sum(mean_mixed * mean_mixed, axis=0, keepdims=True),
        ),
        "model",
    )
    mean_query = mean_query * (jnp.sqrt(own_query) * lax.rsqrt(slope_query_norm + 1e-06))
    mean_key = mean_key * (jnp.sqrt(own_key) * lax.rsqrt(slope_key_norm + 1e-06))
    mean_value = mean_value * (jnp.sqrt(own_value) * lax.rsqrt(slope_value_norm + 1e-06))
    mean_mixed = mean_mixed * (jnp.sqrt(own_mixed) * lax.rsqrt(slope_mixed_norm + 1e-06))
    state_new_query = hold_rate * memory_query + (1.0 - hold_rate) * mean_query * mean_query
    stepped_query = master_query - learn_rate * mean_query * lax.rsqrt(state_new_query + 1e-06)
    state_new_key = hold_rate * memory_key + (1.0 - hold_rate) * mean_key * mean_key
    stepped_key = master_key - learn_rate * mean_key * lax.rsqrt(state_new_key + 1e-06)
    state_new_value = hold_rate * memory_value + (1.0 - hold_rate) * mean_value * mean_value
    stepped_value = master_value - learn_rate * mean_value * lax.rsqrt(state_new_value + 1e-06)
    state_new_mixed = hold_rate * memory_mixed + (1.0 - hold_rate) * mean_mixed * mean_mixed
    stepped_mixed = master_mixed - learn_rate * mean_mixed * lax.rsqrt(state_new_mixed + 1e-06)
    state_new_norm = hold_rate * memory_norm + (1.0 - hold_rate) * mean_norm * mean_norm
    stepped_norm = master_norm - learn_rate * mean_norm * lax.rsqrt(state_new_norm + 1e-06)
    state_new_bias = hold_rate * memory_bias + (1.0 - hold_rate) * mean_bias * mean_bias
    stepped_bias = master_bias - learn_rate * mean_bias * lax.rsqrt(state_new_bias + 1e-06)
    compute_query, compute_key, compute_value, compute_mixed, compute_norm, compute_bias = (
        gather_turned(
            (
                stepped_query.astype(jnp.bfloat16),
                stepped_key.astype(jnp.bfloat16),
                stepped_value.astype(jnp.bfloat16),
                stepped_mixed.astype(jnp.bfloat16),
                stepped_norm.astype(jnp.bfloat16),
                stepped_bias.astype(jnp.bfloat16),
            ),
            REPLICA,
            (0, 0, 0, 1, 0, 0),
        )
    )
    return (
        compute_query,
        compute_key,
        compute_value,
        compute_mixed,
        compute_norm,
        compute_bias,
        stepped_query,
        stepped_key,
        stepped_value,
        stepped_mixed,
        stepped_norm,
        stepped_bias,
        state_new_query,
        state_new_key,
        state_new_value,
        state_new_mixed,
        state_new_norm,
        state_new_bias,
    )


def solution(mesh):
    split = Mesh(
        mesh.devices.reshape(2, 4, 2, mesh.shape["model"]),
        ("replica_0", "replica_1", "replica_2", "model"),
    )
    return jax.shard_map(
        shards,
        mesh=split,
        in_specs=(
            P(REPLICA, None, "model"),
            P(REPLICA, None, "model"),
            P(REPLICA, None, "model"),
            P(REPLICA, "model", None),
            P(REPLICA, None),
            P(REPLICA, None),
            P(REPLICA, "model"),
            P(REPLICA, "model"),
            P(REPLICA, "model"),
            P("model", REPLICA),
            P(REPLICA),
            P(REPLICA),
            P(REPLICA, "model"),
            P(REPLICA, "model"),
            P(REPLICA, "model"),
            P("model", REPLICA),
            P(REPLICA),
            P(REPLICA),
        ),
        out_specs=(
            P(None, "model"),
            P(None, "model"),
            P(None, "model"),
            P("model", None),
            P(),
            P(),
            P(REPLICA, "model"),
            P(REPLICA, "model"),
            P(REPLICA, "model"),
            P("model", REPLICA),
            P(REPLICA),
            P(REPLICA),
            P(REPLICA, "model"),
            P(REPLICA, "model"),
            P(REPLICA, "model"),
            P("model", REPLICA),
            P(REPLICA),
            P(REPLICA),
        ),
        check_vma=False,
    )
```

profile of v0, /device:TPU:1, one launch (start us, length us, event | category | flops | bytes accessed | tf_op | source)
XLA Modules:
  0.0 159.4 jit_solution(13763253603055868574)
XLA Ops:
  7.2 1.3 copy.166
  8.5 6.4 %all-to-all-start.5 = ((f32[2,8,128]{2,1,0:T(8,128)}), f32[2,8,128]{2,1,0:T(8,128)S(1)}, u32[]{:S(2)}, u32[]{:S(2)}) async-start(f32[2,8,128]{2,1,0:T(8,128)} %copy.166), calls=%async_computation.5 | async-start | bytes 16384 | tf_op jit(solution)/shard_map/all_to_all | solution.py:19
  14.9 2.1 %maximum_bitcast_fusion = f32[2,8,128,384]{3,2,0,1:T(8,128)S(1)} fusion(f32[8,2,128,128]{3,2,1,0:T(8,128)} %bitcast.29, f32[8,2,128,128]{3,2,1,0:T(8,128)} %bitcast.30, f32[8,2,128,128]{3,2,1,0:T(8,128)} %bitcast.31), kind=kLoop, calls=%fused_computation | loop fusion | flops 1572864 | bytes 6291456 | tf_op jit(solution)/shard_map/transpose | solution.py:14
  17.0 1.9 %copy.142 = f32[2,8,128,384]{3,2,1,0:T(8,128)} copy(f32[2,8,128,384]{3,2,0,1:T(8,128)S(1)} %maximum_bitcast_fusion) | data formatting | bytes 6291456 | tf_op jit(solution)/shard_map/transpose | solution.py:14
  18.9 0.3 copy.146
  19.2 1.3 copy.147
  20.6 4.0 %all-to-all-start = ((f32[2,8,128,384]{3,2,1,0:T(8,128)}), f32[2,8,128,384]{3,2,1,0:T(8,128)S(1)}, u32[]{:S(2)}, u32[]{:S(2)}) async-start(f32[2,8,128,384]{3,2,1,0:T(8,128)} %copy.142), calls=%async_computation | async-start | bytes 6291456 | tf_op jit(solution)/shard_map/all_to_all | solution.py:19
  24.5 0.6 reduce_sum.166
  25.1 2.7 %all-to-all-done = f32[2,8,128,384]{3,2,1,0:T(8,128)S(1)} async-done(((f32[2,8,128,384]{3,2,1,0:T(8,128)}), f32[2,8,128,384]{3,2,1,0:T(8,128)S(1)}, u32[]{:S(2)}, u32[]{:S(2)}) %all-to-all-start) | async-done | bytes 3145760 | tf_op jit(solution)/shard_map/all_to_all | solution.py:19
  27.8 6.6 %all_to_all.54 = f32[2,8,128,128]{3,1,2,0:T(8,128)} all-to-all(f32[2,8,128,128]{3,1,2,0:T(8,128)} %copy.147), channel_id=1, replica_groups=mesh['replica_0'=2,'replica_1'=4,'replica_2'=2,'model'=16] {'replica_2'}, dimensions={0} | all-to-all | bytes 2097152 | tf_op jit(solution)/shard_map/all_to_all | solution.py:19
  34.3 3.7 %all_to_all.55 = f32[2,8,128]{2,1,0:T(8,128)S(1)} all-to-all(f32[2,8,128]{2,1,0:T(8,128)S(1)} %copy.167), channel_id=1, replica_groups=mesh['replica_0'=2,'replica_1'=4,'replica_2'=2,'model'=16] {'replica_2'}, dimensions={0} | all-to-all | bytes 16384 | tf_op jit(solution)/shard_map/all_to_all | solution.py:19
  38.1 3.8 %all-to-all-start.6 = ((f32[8,1,128]{2,1,0:T(1,128)}), f32[8,1,128]{2,1,0:T(1,128)S(1)}, u32[]{:S(2)}, u32[]{:S(2)}) async-start(f32[8,1,128]{2,1,0:T(1,128)} %bitcast.11), calls=%async_computation.6 | async-start | bytes 8192 | tf_op jit(solution)/shard_map/all_to_all | solution.py:26
  41.9 0.6 reduce_sum.168
  42.5 4.4 %all-to-all-done.6 = f32[8,1,128]{2,1,0:T(1,128)S(1)} async-done(((f32[8,1,128]{2,1,0:T(1,128)}), f32[8,1,128]{2,1,0:T(1,128)S(1)}, u32[]{:S(2)}, u32[]{:S(2)}) %all-to-all-start.6) | async-done | bytes 4128 | tf_op jit(solution)/shard_map/all_to_all | solution.py:26
  46.9 3.3 %all-to-all-start.8 = ((f32[8,1,128]{2,1,0:T(1,128)}), f32[8,1,128]{2,1,0:T(1,128)S(1)}, u32[]{:S(2)}, u32[]{:S(2)}) async-start(f32[8,1,128]{2,1,0:T(1,128)} %bitcast.15), calls=%async_computation.8 | async-start | bytes 8192 | tf_op jit(solution)/shard_map/all_to_all | solution.py:26
  50.2 2.1 %reduce_sum.162 = f32[8,128,128]{2,0,1:T(8,128)} reduce(f32[2,8,128,128]{3,1,2,0:T(8,128)} %all_to_all.54, f32[]{:T(128)} %constant.8.clone.1), dimensions={0}, to_apply=%region_9.0 | reduce | flops 131072 | bytes 1572868 | tf_op jit(solution)/shard_map/reduce_sum | solution.py:20
  52.3 1.9 %copy.149 = f32[8,128,128]{2,1,0:T(8,128)} copy(f32[8,128,128]{2,0,1:T(8,128)} %reduce_sum.162) | data formatting | bytes 1048576 | tf_op jit(solution)/shard_map/reduce_sum | solution.py:20
  54.3 0.8 all-to-all-done.8
  55.1 4.3 %all-to-all-start.3 = ((f32[8,128,128]{2,1,0:T(8,128)}), f32[8,128,128]{2,1,0:T(8,128)}, u32[]{:S(2)}, u32[]{:S(2)}) async-start(f32[8,128,128]{2,1,0:T(8,128)} %copy.149), calls=%async_computation.3 | async-start | bytes 1048576 | tf_op jit(solution)/shard_map/all_to_all | solution.py:26
  59.4 1.5 reduce_sum.153
  60.9 5.7 %all-to-all-done.3 = f32[8,128,128]{2,1,0:T(8,128)} async-done(((f32[8,128,128]{2,1,0:T(8,128)}), f32[8,128,128]{2,1,0:T(8,128)}, u32[]{:S(2)}, u32[]{:S(2)}) %all-to-all-start.3) | async-done | bytes 524320 | tf_op jit(solution)/shard_map/all_to_all | solution.py:26
  66.6 3.6 %all-to-all-start.1 = ((f32[8,128,384]{2,1,0:T(8,128)}), f32[8,128,384]{2,1,0:T(8,128)S(1)}, u32[]{:S(2)}, u32[]{:S(2)}) async-start(f32[8,128,384]{2,1,0:T(8,128)} %reduce_sum.153), calls=%async_computation.1 | async-start | bytes 3145728 | tf_op jit(solution)/shard_map/all_to_all | solution.py:26
  70.2 0.1 copy.157
  70.3 0.1 copy.160
  70.4 0.1 copy.154
  70.5 0.1 copy.155
  70.6 0.1 copy.164
  70.7 0.1 copy.165
  71.0 0.1 copy.153
  71.0 0.1 multiply_reduce_fusion.7
  71.2 0.1 multiply_reduce_fusion.6
  71.3 0.1 multiply_reduce_fusion.5
  71.5 0.5 convert_bitcast_fusion.2
  72.0 0.1 copy.170
  72.2 1.1 reduce_sum.163
  73.3 0.1 copy.150
  73.4 0.1 multiply_reduce_fusion
  73.5 13.5 %all-to-all-done.1 = f32[8,128,384]{2,1,0:T(8,128)S(1)} async-done(((f32[8,128,384]{2,1,0:T(8,128)}), f32[8,128,384]{2,1,0:T(8,128)S(1)}, u32[]{:S(2)}, u32[]{:S(2)}) %all-to-all-start.1) | async-done | bytes 1572896 | tf_op jit(solution)/shard_map/all_to_all | solution.py:26
  87.1 0.1 copy.181
  87.3 0.1 copy.182
  87.4 0.1 copy.145
  87.6 0.7 broadcast_in_dim.3
  88.2 9.9 %all-to-all-start.4 = ((f32[16,1,1024]{2,1,0:T(1,128)}), f32[16,1,1024]{2,1,0:T(1,128)S(1)}, u32[]{:S(2)}, u32[]{:S(2)}) async-start(f32[16,1,1024]{2,1,0:T(1,128)} %broadcast_in_dim.3), calls=%async_computation.4 | async-start | bytes 131072 | tf_op jit(solution)/shard_map/all_to_all | solution.py:38
  98.2 0.5 convert_bitcast_fusion.1
  98.7 0.1 copy.171
  98.8 8.2 %all-to-all-done.4 = f32[16,1,1024]{2,1,0:T(1,128)S(1)} async-done(((f32[16,1,1024]{2,1,0:T(1,128)}), f32[16,1,1024]{2,1,0:T(1,128)S(1)}, u32[]{:S(2)}, u32[]{:S(2)}) %all-to-all-start.4) | async-done | bytes 65568 | tf_op jit(solution)/shard_map/all_to_all | solution.py:38
  107.2 0.1 copy.156
  107.3 0.1 copy.159
  107.4 0.1 copy.162
  107.5 0.1 convert_bitcast_fusion
  107.6 0.1 copy.169
  107.8 0.1 copy.168
  107.9 0.8 fusion.3
  108.7 0.8 concatenate.21
  109.4 0.7 copy.174
  110.2 0.7 copy.175
  110.9 0.7 copy.177
  111.6 0.7 copy.178
  112.4 0.7 copy.173
  113.1 0.7 copy.176
  113.8 32.6 %all-gather.2.cloned.1.call-done = bf16[2048,514]{1,0:T(8,128)(2,1)} async-done(((bf16[128,514]{1,0:T(8,128)(2,1)}), bf16[2048,514]{1,0:T(8,128)(2,1)}) %all-gather.2.cloned.1.call-update) | async-done | bytes 2105360 | tf_op jit(solution)/shard_map/all_gather | solution.py:56
  146.4 2.7 %slice_bitcast_fusion = (bf16[128,2048]{0,1:T(8,128)(2,1)S(1)}, bf16[2048,128]{1,0:T(8,128)(2,1)}, bf16[2048,128]{1,0:T(8,128)(2,1)}, bf16[2048,128]{1,0:T(8,128)(2,1)}) fusion(bf16[2048,514]{1,0:T(8,128)(2,1)} %all-gather.2.cloned.1.call-done), kind=kLoop, calls=%fused_computation.3 | loop fusion | bytes 4194304 | tf_op jit(solution)/shard_map/transpose | solution.py:59
  149.1 1.0 copy.172
  150.1 2.5 %slice_reduce_fusion = (bf16[2048]{0:T(1024)(128)(2,1)}, bf16[2048]{0:T(1024)(128)(2,1)}) fusion(bf16[2048,514]{1,0:T(8,128)(2,1)} %all-gather.2.cloned.1.call-done), kind=kLoop, calls=%fused_computation.1 | loop fusion | bytes 16384 | tf_op jit(solution)/shard_map/slice | solution.py:58
  (56 shorter events, 0.8 us)
Async XLA Ops:
  8.5 12.1 %all-to-all-start.5 = ((f32[2,8,128]{2,1,0:T(8,128)}), f32[2,8,128]{2,1,0:T(8,128)S(1)}, u32[]{:S(2)}, u32[]{:S(2)}) async-start(f32[2,8,128]{2,1,0:T(8,128)} %copy.166), calls=%async_computation.5 | async-start | bytes 16384 | tf_op jit(solution)/shard_map/all_to_all | solution.py:19
  17.0 1.9 %copy-start = (f32[1,128,2048]{2,1,0:T(8,128)S(1)}, f32[1,128,2048]{2,1,0:T(8,128)}, u32[]{:S(2)}) copy-start(f32[1,128,2048]{2,1,0:T(8,128)} %param.21) | copy-start | bytes 3145732
  18.9 1.7 %copy-start.9 = (f32[1,2048]{1,0:T(1,128)S(1)}, f32[1,2048]{1,0:T(1,128)}, u32[]{:S(2)}) copy-start(f32[1,2048]{1,0:T(1,128)} %param.23) | copy-start | bytes 24580
  20.6 7.2 %all-to-all-start = ((f32[2,8,128,384]{3,2,1,0:T(8,128)}), f32[2,8,128,384]{3,2,1,0:T(8,128)S(1)}, u32[]{:S(2)}, u32[]{:S(2)}) async-start(f32[2,8,128,384]{3,2,1,0:T(8,128)} %copy.142), calls=%async_computation | async-start | bytes 6291456 | tf_op jit(solution)/shard_map/all_to_all | solution.py:19
  38.1 8.8 %all-to-all-start.6 = ((f32[8,1,128]{2,1,0:T(1,128)}), f32[8,1,128]{2,1,0:T(1,128)S(1)}, u32[]{:S(2)}, u32[]{:S(2)}) async-start(f32[8,1,128]{2,1,0:T(1,128)} %bitcast.11), calls=%async_computation.6 | async-start | bytes 8192 | tf_op jit(solution)/shard_map/all_to_all | solution.py:26
  46.9 8.2 %all-to-all-start.8 = ((f32[8,1,128]{2,1,0:T(1,128)}), f32[8,1,128]{2,1,0:T(1,128)S(1)}, u32[]{:S(2)}, u32[]{:S(2)}) async-start(f32[8,1,128]{2,1,0:T(1,128)} %bitcast.15), calls=%async_computation.8 | async-start | bytes 8192 | tf_op jit(solution)/shard_map/all_to_all | solution.py:26
  55.1 11.5 %all-to-all-start.3 = ((f32[8,128,128]{2,1,0:T(8,128)}), f32[8,128,128]{2,1,0:T(8,128)}, u32[]{:S(2)}, u32[]{:S(2)}) async-start(f32[8,128,128]{2,1,0:T(8,128)} %copy.149), calls=%async_computation.3 | async-start | bytes 1048576 | tf_op jit(solution)/shard_map/all_to_all | solution.py:26
  59.3 10.9 %copy-start.5 = (f32[128,128]{1,0:T(8,128)S(1)}, f32[128,128]{1,0:T(8,128)}, u32[]{:S(2)}) copy-start(f32[128,128]{1,0:T(8,128)} %param.32) | copy-start | bytes 196612
  59.3 11.1 %copy-start.6 = (f32[128,128]{1,0:T(8,128)S(1)}, f32[128,128]{1,0:T(8,128)}, u32[]{:S(2)}) copy-start(f32[128,128]{1,0:T(8,128)} %param.31) | copy-start | bytes 196612
  59.4 11.2 %copy-start.3 = (f32[128,128]{1,0:T(8,128)S(1)}, f32[128,128]{1,0:T(8,128)}, u32[]{:S(2)}) copy-start(f32[128,128]{1,0:T(8,128)} %param.25) | copy-start | bytes 196612
  59.4 11.3 %copy-start.7 = (f32[128,128]{1,0:T(8,128)S(1)}, f32[128,128]{1,0:T(8,128)}, u32[]{:S(2)}) copy-start(f32[128,128]{1,0:T(8,128)} %param.33) | copy-start | bytes 196612
  60.9 9.8 %copy-start.4 = (f32[128,128]{1,0:T(8,128)S(1)}, f32[128,128]{1,0:T(8,128)}, u32[]{:S(2)}) copy-start(f32[128,128]{1,0:T(8,128)} %param.27) | copy-start | bytes 196612
  60.9 9.9 %copy-start.8 = (f32[128,128]{1,0:T(8,128)S(1)}, f32[128,128]{1,0:T(8,128)}, u32[]{:S(2)}) copy-start(f32[128,128]{1,0:T(8,128)} %param.30) | copy-start | bytes 196612
  60.9 10.1 %copy-start.2 = (f32[128,128]{1,0:T(8,128)S(1)}, f32[128,128]{1,0:T(8,128)}, u32[]{:S(2)}) copy-start(f32[128,128]{1,0:T(8,128)} %param.24) | copy-start | bytes 196612
  60.9 10.4 %copy-start.1 = (f32[128,128]{1,0:T(8,128)S(1)}, f32[128,128]{1,0:T(8,128)}, u32[]{:S(2)}) copy-start(f32[128,128]{1,0:T(8,128)} %param.26) | copy-start | bytes 196612
  60.9 10.6 %copy-start.10 = (f32[128]{0:T(128)S(1)}, f32[128]{0:T(128)}, u32[]{:S(2)}) copy-start(f32[128]{0:T(128)} %param.28) | copy-start | bytes 1540
  60.9 10.6 %copy-start.11 = (f32[128]{0:T(128)S(1)}, f32[128]{0:T(128)}, u32[]{:S(2)}) copy-start(f32[128]{0:T(128)} %param.34) | copy-start | bytes 1540
  66.6 20.4 %all-to-all-start.1 = ((f32[8,128,384]{2,1,0:T(8,128)}), f32[8,128,384]{2,1,0:T(8,128)S(1)}, u32[]{:S(2)}, u32[]{:S(2)}) async-start(f32[8,128,384]{2,1,0:T(8,128)} %reduce_sum.153), calls=%async_computation.1 | async-start | bytes 3145728 | tf_op jit(solution)/shard_map/all_to_all | solution.py:26
  70.2 28.0 %copy-start.12 = (f32[128]{0:T(128)S(1)}, f32[128]{0:T(128)}, u32[]{:S(2)}) copy-start(f32[128]{0:T(128)} %param.29) | copy-start | bytes 1540
  70.2 28.0 %copy-start.13 = (f32[128]{0:T(128)S(1)}, f32[128]{0:T(128)}, u32[]{:S(2)}) copy-start(f32[128]{0:T(128)} %param.35) | copy-start | bytes 1540
  88.2 18.8 %all-to-all-start.4 = ((f32[16,1,1024]{2,1,0:T(1,128)}), f32[16,1,1024]{2,1,0:T(1,128)S(1)}, u32[]{:S(2)}, u32[]{:S(2)}) async-start(f32[16,1,1024]{2,1,0:T(1,128)} %broadcast_in_dim.3), calls=%async_computation.4 | async-start | bytes 131072 | tf_op jit(solution)/shard_map/all_to_all | solution.py:38
  98.1 48.3 %all-gather.2.cloned.1.call-start = ((), (), s32[]{:S(2)}) async-start(), calls=%async_computation.9 | async-start | bytes 2785280 | tf_op jit(solution)/shard_map/all_gather | solution.py:56
Sparse Core Ops, SparseCore 0:
  109.6 36.7 all-gather.1
where the time goes:
time: 160 us; the launch traced here: 159 us
  waiting for transfers between devices  67.8 us (42%)
  starting transfers between devices  35.3 us (22%)
  local copies, waits for them, and re-layouts  20.7 us (13%)
  between operations  14.5 us (9%)
  other arithmetic  10.8 us (7%)
  blocking collectives  10.3 us (6%)
    all_gather x1, waiting for transfers between devices, gather_turned(): out, at, outs = (lax.all_gather(both, axis, axis=0, tiled=True), 0, [])  32.6 us
    all_to_all x4, waiting for transfers between devices, sum_by_axis(): return jnp.sum(lax.all_to_all(own, far, 0, 0, tiled=True), axis=0)  24.4 us
    all_to_all x4, starting transfers between devices, sum_by_axis(): return jnp.sum(lax.all_to_all(own, far, 0, 0, tiled=True), axis=0)  15 us
    all_to_all x2, starting transfers between devices, sum_at_owner(): blocks = lax.all_to_all(cut_along(x, dim, size), axis, 0, 0, tiled=True)  10.4 us
    all_to_all x2, blocking collectives, sum_at_owner(): blocks = lax.all_to_all(cut_along(x, dim, size), axis, 0, 0, tiled=True)  10.3 us
    all_to_all x1, starting transfers between devices, copy_for_each(): return lax.all_to_all(copies, axis, split_axis=0, concat_axis=0, tiled=True)  9.85 us
    all_to_all x1, waiting for transfers between devices, copy_for_each(): return lax.all_to_all(copies, axis, split_axis=0, concat_axis=0, tiled=True)  8.2 us
    unnamed x52, local copies, waits for them, and re-layouts  6.61 us
  transfers between devices with their start and end apart: 8, of which 7 were waited for; matrix products, arithmetic and copies ran while one was open for 13% of the time, Pallas kernels for 0%

commit v1 on v0

--- a/solution.py
+++ b/solution.py
@@ -53,7 +53,13 @@
 def gather_turned(arrays, axis, dims):
     turned = [jnp.moveaxis(a, dim, 0) for a, dim in zip(arrays, dims)]
     both = jnp.concatenate([t.reshape(len(t), -1) for t in turned], axis=1)
-    out, at, outs = (lax.all_gather(both, axis, axis=0, tiled=True), 0, [])
+    out, at, outs = (
+        jnp.concatenate(
+            lax.all_to_all(jnp.stack([both] * lax.axis_size(axis)), axis, 0, 0), axis=0
+        ),
+        0,
+        [],
+    )
     for t, dim in zip(turned, dims):
         share = out[:, at : at + t[0].size].reshape(-1, *t.shape[1:])
         outs.append(jnp.moveaxis(share, 0, dim))

time: 160 us -> 149 us (0.931)
  between operations: 14.5 us -> 1.17 us
  starting transfers between devices: 35.3 us -> 44.7 us
  waiting for transfers between devices: 67.8 us -> 58.9 us
    all_gather x1 -> x0, waiting for transfers between devices: 32.6 us -> none  [gather_turned(): out, at, outs = (lax.all_gather(both, axis, axis=0, tiled=True), 0, [])]
    all_to_all x0 -> x1, waiting for transfers between devices: none -> 23.7 us  [gather_turned(): lax.all_to_all(jnp.stack([both] * lax.axis_size(axis)), axis, 0, 0)]
    all_to_all x0 -> x1, starting transfers between devices: none -> 9.45 us  [gather_turned(): lax.all_to_all(jnp.stack([both] * lax.axis_size(axis)), axis, 0, 0)]
    unnamed x52 -> x56, local copies, waits for them, and re-layouts: 6.61 us -> 9.52 us
    slice x1, local copies, waits for them, and re-layouts: 2.46 us -> 0.64 us  [gather_turned(): share = out[:, at:at + t[0].size].reshape(-1, *t.shape[1:])]
    transpose x1, local copies, waits for them, and re-layouts: 2.74 us -> 1.01 us  [gather_turned(): outs.append(jnp.moveaxis(share, 0, dim))]
    another operation x0 -> x1, local copies, waits for them, and re-layouts: none -> 1.63 us  [gather_turned(): jnp.stack([both] * lax.axis_size(axis))]
  transfers between devices with their start and end apart: 8 -> 8, of which waited for: 7 -> 7; matrix products, arithmetic and copies ran while one was open for 13% -> 14% of each run, Pallas kernels for 0% -> 0%
where the time goes in v1:
time: 149 us; the launch traced here: 147 us
  waiting for transfers between devices  58.9 us (40%)
  starting transfers between devices  44.7 us (30%)
  local copies, waits for them, and re-layouts  21.5 us (14%)
  other arithmetic  10.8 us (7%)
  blocking collectives  10.3 us (7%)
    all_to_all x4, waiting for transfers between devices, sum_by_axis(): return jnp.sum(lax.all_to_all(own, far, 0, 0, tiled=True), axis=0)  24.4 us
    all_to_all x1, waiting for transfers between devices, gather_turned(): lax.all_to_all(jnp.stack([both] * lax.axis_size(axis)), axis, 0, 0)  23.7 us
    all_to_all x4, starting transfers between devices, sum_by_axis(): return jnp.sum(lax.all_to_all(own, far, 0, 0, tiled=True), axis=0)  15 us
    all_to_all x2, starting transfers between devices, sum_at_owner(): blocks = lax.all_to_all(cut_along(x, dim, size), axis, 0, 0, tiled=True)  10.4 us
    all_to_all x2, blocking collectives, sum_at_owner(): blocks = lax.all_to_all(cut_along(x, dim, size), axis, 0, 0, tiled=True)  10.3 us
    all_to_all x1, starting transfers between devices, copy_for_each(): return lax.all_to_all(copies, axis, split_axis=0, concat_axis=0, tiled=True)  9.85 us
    unnamed x56, local copies, waits for them, and re-layouts  9.52 us
    all_to_all x1, starting transfers between devices, gather_turned(): lax.all_to_all(jnp.stack([both] * lax.axis_size(axis)), axis, 0, 0)  9.45 us
  transfers between devices with their start and end apart: 8, of which 7 were waited for; matrix products, arithmetic and copies ran while one was open for 14% of the time, Pallas kernels for 0%

profile of v1, /device:TPU:1, one launch (start us, length us, event | category | flops | bytes accessed | tf_op | source)
XLA Modules:
  0.0 147.4 jit_solution(17260735549495999148)
XLA Ops:
  0.7 1.3 copy.138
  2.0 6.4 %all-to-all-start.5 = ((f32[2,8,128]{2,1,0:T(8,128)}), f32[2,8,128]{2,1,0:T(8,128)S(1)}, u32[]{:S(2)}, u32[]{:S(2)}) async-start(f32[2,8,128]{2,1,0:T(8,128)} %copy.138), calls=%async_computation.5 | async-start | bytes 16384 | tf_op jit(solution)/shard_map/all_to_all | solution.py:19
  8.4 2.1 %maximum_bitcast_fusion = f32[2,8,128,384]{3,2,0,1:T(8,128)S(1)} fusion(f32[8,2,128,128]{3,2,1,0:T(8,128)} %bitcast.40, f32[8,2,128,128]{3,2,1,0:T(8,128)} %bitcast.41, f32[8,2,128,128]{3,2,1,0:T(8,128)} %bitcast.42), kind=kLoop, calls=%fused_computation | loop fusion | flops 1572864 | bytes 6291456 | tf_op jit(solution)/shard_map/transpose | solution.py:14
  10.5 1.9 %copy.114 = f32[2,8,128,384]{3,2,1,0:T(8,128)} copy(f32[2,8,128,384]{3,2,0,1:T(8,128)S(1)} %maximum_bitcast_fusion) | data formatting | bytes 6291456 | tf_op jit(solution)/shard_map/transpose | solution.py:14
  12.4 0.3 copy.118
  12.7 1.3 copy.119
  14.0 4.0 %all-to-all-start = ((f32[2,8,128,384]{3,2,1,0:T(8,128)}), f32[2,8,128,384]{3,2,1,0:T(8,128)S(1)}, u32[]{:S(2)}, u32[]{:S(2)}) async-start(f32[2,8,128,384]{3,2,1,0:T(8,128)} %copy.114), calls=%async_computation | async-start | bytes 6291456 | tf_op jit(solution)/shard_map/all_to_all | solution.py:19
  18.0 0.6 reduce_sum.166
  18.6 2.7 %all-to-all-done = f32[2,8,128,384]{3,2,1,0:T(8,128)S(1)} async-done(((f32[2,8,128,384]{3,2,1,0:T(8,128)}), f32[2,8,128,384]{3,2,1,0:T(8,128)S(1)}, u32[]{:S(2)}, u32[]{:S(2)}) %all-to-all-start) | async-done | bytes 3145760 | tf_op jit(solution)/shard_map/all_to_all | solution.py:19
  21.2 6.6 %all_to_all.59 = f32[2,8,128,128]{3,1,2,0:T(8,128)} all-to-all(f32[2,8,128,128]{3,1,2,0:T(8,128)} %copy.119), channel_id=1, replica_groups=mesh['replica_0'=2,'replica_1'=4,'replica_2'=2,'model'=16] {'replica_2'}, dimensions={0} | all-to-all | bytes 2097152 | tf_op jit(solution)/shard_map/all_to_all | solution.py:19
  27.8 3.7 %all_to_all.60 = f32[2,8,128]{2,1,0:T(8,128)S(1)} all-to-all(f32[2,8,128]{2,1,0:T(8,128)S(1)} %copy.139), channel_id=1, replica_groups=mesh['replica_0'=2,'replica_1'=4,'replica_2'=2,'model'=16] {'replica_2'}, dimensions={0} | all-to-all | bytes 16384 | tf_op jit(solution)/shard_map/all_to_all | solution.py:19
  31.5 3.8 %all-to-all-start.6 = ((f32[8,1,128]{2,1,0:T(1,128)}), f32[8,1,128]{2,1,0:T(1,128)S(1)}, u32[]{:S(2)}, u32[]{:S(2)}) async-start(f32[8,1,128]{2,1,0:T(1,128)} %bitcast.11), calls=%async_computation.6 | async-start | bytes 8192 | tf_op jit(solution)/shard_map/all_to_all | solution.py:26
  35.4 0.6 reduce_sum.168
  36.0 4.4 %all-to-all-done.6 = f32[8,1,128]{2,1,0:T(1,128)S(1)} async-done(((f32[8,1,128]{2,1,0:T(1,128)}), f32[8,1,128]{2,1,0:T(1,128)S(1)}, u32[]{:S(2)}, u32[]{:S(2)}) %all-to-all-start.6) | async-done | bytes 4128 | tf_op jit(solution)/shard_map/all_to_all | solution.py:26
  40.3 3.3 %all-to-all-start.8 = ((f32[8,1,128]{2,1,0:T(1,128)}), f32[8,1,128]{2,1,0:T(1,128)S(1)}, u32[]{:S(2)}, u32[]{:S(2)}) async-start(f32[8,1,128]{2,1,0:T(1,128)} %bitcast.15), calls=%async_computation.8 | async-start | bytes 8192 | tf_op jit(solution)/shard_map/all_to_all | solution.py:26
  43.7 2.1 %reduce_sum.162 = f32[8,128,128]{2,0,1:T(8,128)} reduce(f32[2,8,128,128]{3,1,2,0:T(8,128)} %all_to_all.59, f32[]{:T(128)} %constant.8.clone.1), dimensions={0}, to_apply=%region_9.0 | reduce | flops 131072 | bytes 1572868 | tf_op jit(solution)/shard_map/reduce_sum | solution.py:20
  45.8 1.9 %copy.121 = f32[8,128,128]{2,1,0:T(8,128)} copy(f32[8,128,128]{2,0,1:T(8,128)} %reduce_sum.162) | data formatting | bytes 1048576 | tf_op jit(solution)/shard_map/reduce_sum | solution.py:20
  47.7 0.8 all-to-all-done.8
  48.5 4.3 %all-to-all-start.3 = ((f32[8,128,128]{2,1,0:T(8,128)}), f32[8,128,128]{2,1,0:T(8,128)}, u32[]{:S(2)}, u32[]{:S(2)}) async-start(f32[8,128,128]{2,1,0:T(8,128)} %copy.121), calls=%async_computation.3 | async-start | bytes 1048576 | tf_op jit(solution)/shard_map/all_to_all | solution.py:26
  52.8 1.5 %reduce_sum.153 = f32[8,128,384]{2,1,0:T(8,128)} reduce(f32[2,8,128,384]{3,2,1,0:T(8,128)S(1)} %all-to-all-done, f32[]{:T(128)} %constant.8.clone.1), dimensions={0}, to_apply=%region_0.0 | reduce | flops 393216 | bytes 4718596 | tf_op jit(solution)/shard_map/reduce_sum | solution.py:20
  54.4 5.7 %all-to-all-done.3 = f32[8,128,128]{2,1,0:T(8,128)} async-done(((f32[8,128,128]{2,1,0:T(8,128)}), f32[8,128,128]{2,1,0:T(8,128)}, u32[]{:S(2)}, u32[]{:S(2)}) %all-to-all-start.3) | async-done | bytes 524320 | tf_op jit(solution)/shard_map/all_to_all | solution.py:26
  60.0 3.6 %all-to-all-start.1 = ((f32[8,128,384]{2,1,0:T(8,128)}), f32[8,128,384]{2,1,0:T(8,128)S(1)}, u32[]{:S(2)}, u32[]{:S(2)}) async-start(f32[8,128,384]{2,1,0:T(8,128)} %reduce_sum.153), calls=%async_computation.1 | async-start | bytes 3145728 | tf_op jit(solution)/shard_map/all_to_all | solution.py:26
  63.6 0.1 copy.129
  63.8 0.1 copy.132
  64.5 0.1 multiply_reduce_fusion.7
  64.6 0.1 multiply_reduce_fusion.6
  64.8 0.1 multiply_reduce_fusion.5
  65.0 0.5 convert_bitcast_fusion.2
  65.5 0.1 copy.142
  65.7 1.1 reduce_sum.163
  66.8 0.1 multiply_reduce_fusion
  67.0 13.5 %all-to-all-done.1 = f32[8,128,384]{2,1,0:T(8,128)S(1)} async-done(((f32[8,128,384]{2,1,0:T(8,128)}), f32[8,128,384]{2,1,0:T(8,128)S(1)}, u32[]{:S(2)}, u32[]{:S(2)}) %all-to-all-start.1) | async-done | bytes 1572896 | tf_op jit(solution)/shard_map/all_to_all | solution.py:26
  80.7 0.1 copy.158
  80.9 0.1 copy.117
  81.0 0.7 broadcast_in_dim.3
  81.7 9.9 %all-to-all-start.4 = ((f32[16,1,1024]{2,1,0:T(1,128)}), f32[16,1,1024]{2,1,0:T(1,128)S(1)}, u32[]{:S(2)}, u32[]{:S(2)}) async-start(f32[16,1,1024]{2,1,0:T(1,128)} %broadcast_in_dim.3), calls=%async_computation.4 | async-start | bytes 131072 | tf_op jit(solution)/shard_map/all_to_all | solution.py:38
  91.6 0.5 convert_bitcast_fusion.1
  92.1 0.1 copy.143
  92.3 8.3 %all-to-all-done.4 = f32[16,1,1024]{2,1,0:T(1,128)S(1)} async-done(((f32[16,1,1024]{2,1,0:T(1,128)}), f32[16,1,1024]{2,1,0:T(1,128)S(1)}, u32[]{:S(2)}, u32[]{:S(2)}) %all-to-all-start.4) | async-done | bytes 65568 | tf_op jit(solution)/shard_map/all_to_all | solution.py:38
  100.7 0.1 copy.128
  100.9 0.1 copy.134
  101.0 0.1 convert_bitcast_fusion
  101.1 0.1 copy.141
  101.3 0.1 copy.140
  101.4 0.8 fusion.3
  102.1 0.1 concatenate.21
  102.2 0.1 copy.144
  102.4 1.6 %stack.2 = bf16[16,128,514]{1,2,0:T(8,128)(2,1)} broadcast(bf16[128,514]{0,1:T(8,128)(2,1)S(1)} %copy.144), dimensions={1,2} | broadcast | bytes 2236928 | tf_op jit(solution)/shard_map/stack | solution.py:58
  104.0 9.5 %all-to-all-start.9 = ((bf16[16,128,514]{1,2,0:T(8,128)(2,1)}), bf16[16,128,514]{1,2,0:T(8,128)(2,1)S(1)}, u32[]{:S(2)}, u32[]{:S(2)}) async-start(bf16[16,128,514]{1,2,0:T(8,128)(2,1)} %stack.2), calls=%async_computation.9 | async-start | bytes 4259840 | tf_op jit(solution)/shard_map/all_to_all | solution.py:58
  113.4 0.7 copy.150
  114.2 0.7 copy.151
  114.9 0.7 copy.153
  115.6 0.7 copy.154
  116.4 0.7 copy.149
  117.1 0.7 copy.152
  117.8 23.7 %all-to-all-done.9 = bf16[16,128,514]{1,2,0:T(8,128)(2,1)S(1)} async-done(((bf16[16,128,514]{1,2,0:T(8,128)(2,1)}), bf16[16,128,514]{1,2,0:T(8,128)(2,1)S(1)}, u32[]{:S(2)}, u32[]{:S(2)}) %all-to-all-start.9) | async-done | bytes 2105376 | tf_op jit(solution)/shard_map/all_to_all | solution.py:58
  141.5 0.3 copy.169
  141.8 0.4 pad.3
  142.2 0.6 copy.167
  142.7 1.0 slice_bitcast_fusion
  143.7 0.6 slice_reduce_fusion
  144.4 1.0 copy.146
  145.4 1.0 copy.147
  146.4 1.0 copy.148
  (62 shorter events, 1.4 us)
Async XLA Ops:
  2.0 12.1 %all-to-all-start.5 = ((f32[2,8,128]{2,1,0:T(8,128)}), f32[2,8,128]{2,1,0:T(8,128)S(1)}, u32[]{:S(2)}, u32[]{:S(2)}) async-start(f32[2,8,128]{2,1,0:T(8,128)} %copy.138), calls=%async_computation.5 | async-start | bytes 16384 | tf_op jit(solution)/shard_map/all_to_all | solution.py:19
  10.5 1.9 %copy-start = (f32[1,128,2048]{2,1,0:T(8,128)S(1)}, f32[1,128,2048]{2,1,0:T(8,128)}, u32[]{:S(2)}) copy-start(f32[1,128,2048]{2,1,0:T(8,128)} %param.21) | copy-start | bytes 3145732
  12.4 1.7 %copy-start.9 = (f32[1,2048]{1,0:T(1,128)S(1)}, f32[1,2048]{1,0:T(1,128)}, u32[]{:S(2)}) copy-start(f32[1,2048]{1,0:T(1,128)} %param.23) | copy-start | bytes 24580
  14.0 7.2 %all-to-all-start = ((f32[2,8,128,384]{3,2,1,0:T(8,128)}), f32[2,8,128,384]{3,2,1,0:T(8,128)S(1)}, u32[]{:S(2)}, u32[]{:S(2)}) async-start(f32[2,8,128,384]{3,2,1,0:T(8,128)} %copy.114), calls=%async_computation | async-start | bytes 6291456 | tf_op jit(solution)/shard_map/all_to_all | solution.py:19
  31.5 8.8 %all-to-all-start.6 = ((f32[8,1,128]{2,1,0:T(1,128)}), f32[8,1,128]{2,1,0:T(1,128)S(1)}, u32[]{:S(2)}, u32[]{:S(2)}) async-start(f32[8,1,128]{2,1,0:T(1,128)} %bitcast.11), calls=%async_computation.6 | async-start | bytes 8192 | tf_op jit(solution)/shard_map/all_to_all | solution.py:26
  40.3 8.2 %all-to-all-start.8 = ((f32[8,1,128]{2,1,0:T(1,128)}), f32[8,1,128]{2,1,0:T(1,128)S(1)}, u32[]{:S(2)}, u32[]{:S(2)}) async-start(f32[8,1,128]{2,1,0:T(1,128)} %bitcast.15), calls=%async_computation.8 | async-start | bytes 8192 | tf_op jit(solution)/shard_map/all_to_all | solution.py:26
  48.5 11.5 %all-to-all-start.3 = ((f32[8,128,128]{2,1,0:T(8,128)}), f32[8,128,128]{2,1,0:T(8,128)}, u32[]{:S(2)}, u32[]{:S(2)}) async-start(f32[8,128,128]{2,1,0:T(8,128)} %copy.121), calls=%async_computation.3 | async-start | bytes 1048576 | tf_op jit(solution)/shard_map/all_to_all | solution.py:26
  54.3 9.3 %copy-start.5 = (f32[128,128]{1,0:T(8,128)S(1)}, f32[128,128]{1,0:T(8,128)}, u32[]{:S(2)}) copy-start(f32[128,128]{1,0:T(8,128)} %param.32) | copy-start | bytes 196612
  54.3 9.5 %copy-start.6 = (f32[128,128]{1,0:T(8,128)S(1)}, f32[128,128]{1,0:T(8,128)}, u32[]{:S(2)}) copy-start(f32[128,128]{1,0:T(8,128)} %param.31) | copy-start | bytes 196612
  54.3 9.6 %copy-start.3 = (f32[128,128]{1,0:T(8,128)S(1)}, f32[128,128]{1,0:T(8,128)}, u32[]{:S(2)}) copy-start(f32[128,128]{1,0:T(8,128)} %param.25) | copy-start | bytes 196612
  54.3 9.8 %copy-start.7 = (f32[128,128]{1,0:T(8,128)S(1)}, f32[128,128]{1,0:T(8,128)}, u32[]{:S(2)}) copy-start(f32[128,128]{1,0:T(8,128)} %param.33) | copy-start | bytes 196612
  54.3 9.9 %copy-start.4 = (f32[128,128]{1,0:T(8,128)S(1)}, f32[128,128]{1,0:T(8,128)}, u32[]{:S(2)}) copy-start(f32[128,128]{1,0:T(8,128)} %param.27) | copy-start | bytes 196612
  54.3 10.0 %copy-start.8 = (f32[128,128]{1,0:T(8,128)S(1)}, f32[128,128]{1,0:T(8,128)}, u32[]{:S(2)}) copy-start(f32[128,128]{1,0:T(8,128)} %param.30) | copy-start | bytes 196612
  54.3 10.0 %copy-start.2 = (f32[128,128]{1,0:T(8,128)S(1)}, f32[128,128]{1,0:T(8,128)}, u32[]{:S(2)}) copy-start(f32[128,128]{1,0:T(8,128)} %param.24) | copy-start | bytes 196612
  54.4 10.4 %copy-start.1 = (f32[128,128]{1,0:T(8,128)S(1)}, f32[128,128]{1,0:T(8,128)}, u32[]{:S(2)}) copy-start(f32[128,128]{1,0:T(8,128)} %param.26) | copy-start | bytes 196612
  54.4 10.6 %copy-start.10 = (f32[128]{0:T(128)S(1)}, f32[128]{0:T(128)}, u32[]{:S(2)}) copy-start(f32[128]{0:T(128)} %param.28) | copy-start | bytes 1540
  54.4 10.6 %copy-start.11 = (f32[128]{0:T(128)S(1)}, f32[128]{0:T(128)}, u32[]{:S(2)}) copy-start(f32[128]{0:T(128)} %param.34) | copy-start | bytes 1540
  60.0 20.4 %all-to-all-start.1 = ((f32[8,128,384]{2,1,0:T(8,128)}), f32[8,128,384]{2,1,0:T(8,128)S(1)}, u32[]{:S(2)}, u32[]{:S(2)}) async-start(f32[8,128,384]{2,1,0:T(8,128)} %reduce_sum.153), calls=%async_computation.1 | async-start | bytes 3145728 | tf_op jit(solution)/shard_map/all_to_all | solution.py:26
  64.4 27.2 %copy-start.12 = (f32[128]{0:T(128)S(1)}, f32[128]{0:T(128)}, u32[]{:S(2)}) copy-start(f32[128]{0:T(128)} %param.29) | copy-start | bytes 1540
  64.4 27.2 %copy-start.13 = (f32[128]{0:T(128)S(1)}, f32[128]{0:T(128)}, u32[]{:S(2)}) copy-start(f32[128]{0:T(128)} %param.35) | copy-start | bytes 1540
  81.7 18.8 %all-to-all-start.4 = ((f32[16,1,1024]{2,1,0:T(1,128)}), f32[16,1,1024]{2,1,0:T(1,128)S(1)}, u32[]{:S(2)}, u32[]{:S(2)}) async-start(f32[16,1,1024]{2,1,0:T(1,128)} %broadcast_in_dim.3), calls=%async_computation.4 | async-start | bytes 131072 | tf_op jit(solution)/shard_map/all_to_all | solution.py:38
  104.0 37.5 %all-to-all-start.9 = ((bf16[16,128,514]{1,2,0:T(8,128)(2,1)}), bf16[16,128,514]{1,2,0:T(8,128)(2,1)S(1)}, u32[]{:S(2)}, u32[]{:S(2)}) async-start(bf16[16,128,514]{1,2,0:T(8,128)(2,1)} %stack.2), calls=%async_computation.9 | async-start | bytes 4259840 | tf_op jit(solution)/shard_map/all_to_all | solution.py:58
